TPU v7x, 128 devices: a whole 4x4x4 slice. The times are simulated.
128 devices in a mesh: mat: 4 (over x), row: 8 (over z, y_hi), col: 2 (over core), dep: 2 (over y_lo).
Axes of the slice: x: 4, y: 4 (y_hi: 2, y_lo: 2; y = y_hi * 2 + y_lo), z: 4, core: 2. Of those that a mesh axis runs over, the one named last changes fastest.
Arguments:
- iterate: bfloat16 [8192, 14336], P('mat', ('row', 'col', 'dep')), parts along dimension 0, may hold values from -0.03125 to 0.03125
Outputs:
- update: bfloat16 [8192, 14336], P('mat', ('row', 'col', 'dep')), parts along dimension 0
There are 4 independent parts, one for each index of `mat`. A program takes and returns all parts, laid end to end along the dimension named above; each array names one. Nothing has to cross between parts.
All inputs are finite; a program needn't handle non-finite values.
Results may differ from a plain program's by a relative error of at most 0.0059.
Values may be sent and summed in bfloat16 or wider, within the bound.
A program may use at most 128 MiB of HBM per device.

v0:
```python
import math

import jax
import jax.numpy as jnp
from jax import lax
from jax.sharding import Mesh
from jax.sharding import PartitionSpec as P

FF = 14336
ROW_COL_DEP = ("row_0", "row_1", "col", "dep")


coef_a = 3.4445
coef_b = -4.775
coef_c = 2.0315


def reduced_to_own(tiles, axes, sequence):
    inside = tiles.shape[1:]
    tiles = tiles.reshape(*(lax.axis_size(a) for a in axes), *inside)
    tiles = jnp.moveaxis(tiles, sequence, range(len(axes))).reshape(-1, *inside)
    for k in sequence:
        tiles = lax.psum_scatter(tiles, axes[k], scatter_dimension=0, tiled=True)
    return tiles[0]


def cut_along(array, dim, devices):
    dims = array.shape
    tiles = array.reshape(*dims[:dim], devices, dims[dim] // devices, *dims[dim + 1 :])
    return jnp.moveaxis(tiles, dim, 0)


def sum_by_axis(array, axes, sequence, dim):
    devices = lax.axis_size(axes)
    return reduced_to_own(cut_along(array, dim, devices), axes, sequence)


def square_folder(gram_half, piece):
    return jnp.dot(gram_half, piece, preferred_element_type=jnp.float32)


def body(iterate):
    scale = math.sqrt(FF)
    gram_mine = sum_by_axis(
        lax.dot_general(
            iterate, iterate, (((1,), (1,)), ((), ())), preferred_element_type=jnp.float32
        ),
        ROW_COL_DEP,
        (2, 0, 3, 1),
        0,
    )
    gram_half = gram_mine.astype(jnp.bfloat16)
    square = square_folder(gram_half, lax.all_gather(gram_half, ROW_COL_DEP, axis=0, tiled=True))
    poly = (coef_b * gram_half.astype(jnp.float32) + coef_c * square).astype(jnp.bfloat16)
    applied = jnp.dot(
        lax.all_gather(poly, ROW_COL_DEP, axis=0, tiled=True),
        iterate,
        preferred_element_type=jnp.float32,
    )
    updated = coef_a * iterate.astype(jnp.float32) + applied
    return (scale * updated).astype(jnp.bfloat16)


def solution(mesh):
    torus = Mesh(
        mesh.devices.reshape(mesh.shape["mat"], 4, 2, mesh.shape["col"], mesh.shape["dep"]),
        ("mat", "row_0", "row_1", "col", "dep"),
    )
    in_specs = (P("mat", ROW_COL_DEP),)
    out_specs = P("mat", ROW_COL_DEP)
    return jax.shard_map(body, mesh=torus, in_specs=in_specs, out_specs=out_specs, check_vma=False)
```

profile of v0, /device:TPU:1, one launch (start us, length us, event | category | flops | bytes accessed | tf_op | source)
XLA Modules:
  0.0 407.2 jit_solution(13816291408495255569)
XLA Ops:
  6.5 0.0 reduce-scatter.5.cloned.1.call-start
  6.5 6.7 %fusion.12 = f32[2048,2048]{1,0:T(8,128)S(1)} fusion(bf16[2048,448]{0,1:T(8,128)(2,1)} %param.1), kind=kOutput, calls=%fused_computation.7 | convolution fusion | flops 3758096384 | bytes 18612224 | tf_op jit(solution)/shard_map/dot_general | solution.py:45
  13.2 6.3 %copy.2 = f32[4,2,2,2,64,2048]{5,4,1,3,0,2:T(8,128)} copy(f32[4,2,2,2,64,2048]{5,4,3,2,1,0:T(8,128)S(1)} %bitcast.21) | data formatting | bytes 33554432 | tf_op jit(solution)/shard_map/reshape;reshape | solution.py:20
  19.5 0.0 reduce-scatter.5.cloned.1.call-update
  19.5 0.0 reduce-scatter.7.cloned.1.call-start
  19.6 31.5 %reduce-scatter.5.cloned.1.call-done = f32[16,64,2048]{2,1,0:T(8,128)} async-done(((f32[32,64,2048]{2,1,0:T(8,128)}), f32[16,64,2048]{2,1,0:T(8,128)}) %reduce-scatter.5.cloned.1.call-update) | async-done | bytes 8388624 | tf_op jit(solution)/shard_map/reduce_scatter | solution.py:23
  51.0 0.0 reduce-scatter.7.cloned.1.call-update
  51.0 0.0 reduce-scatter.9.cloned.1.call-start
  51.1 84.2 %reduce-scatter.7.cloned.1.call-done = f32[4,64,2048]{2,1,0:T(8,128)} async-done(((f32[16,64,2048]{2,1,0:T(8,128)}), f32[4,64,2048]{2,1,0:T(8,128)}) %reduce-scatter.7.cloned.1.call-update) | async-done | bytes 2097168 | tf_op jit(solution)/shard_map/reduce_scatter | solution.py:23
  135.3 0.0 reduce-scatter.9.cloned.1.call-update
  135.3 0.0 reduce-scatter.11.cloned.1.call-start
  135.4 36.2 %reduce-scatter.9.cloned.1.call-done = f32[2,64,2048]{2,1,0:T(8,128)} async-done(((f32[4,64,2048]{2,1,0:T(8,128)}), f32[2,64,2048]{2,1,0:T(8,128)}) %reduce-scatter.9.cloned.1.call-update) | async-done | bytes 1048592 | tf_op jit(solution)/shard_map/reduce_scatter | solution.py:23
  171.6 0.0 reduce-scatter.11.cloned.1.call-update
  171.6 0.0 all-gather.6.cloned.1.call-start
  171.7 27.6 %reduce-scatter.11.cloned.1.call-done = f32[1,64,2048]{2,1,0:T(8,128)} async-done(((f32[2,64,2048]{2,1,0:T(8,128)}), f32[1,64,2048]{2,1,0:T(8,128)}) %reduce-scatter.11.cloned.1.call-update) | async-done | bytes 524304 | tf_op jit(solution)/shard_map/reduce_scatter | solution.py:23
  199.3 1.8 convert_element_type.19
  201.0 0.0 all-gather.6.cloned.1.call-update
  201.0 0.0 copy-start
  201.1 0.0 all-gather.4.cloned.1.call-start
  201.1 91.0 %all-gather.6.cloned.1.call-done = bf16[1,2048,2048]{2,1,0:T(8,128)(2,1)} async-done(((bf16[1,64,2048]{2,1,0:T(8,128)(2,1)}), bf16[1,2048,2048]{2,1,0:T(8,128)(2,1)}) %all-gather.6.cloned.1.call-update) | async-done | bytes 8388624 | tf_op jit(solution)/shard_map/all_gather | solution.py:53
  292.1 5.7 %fusion.8 = bf16[64,2048]{1,0:T(8,128)(2,1)} fusion(bf16[1,2048,2048]{2,1,0:T(8,128)(2,1)} %all-gather.6.cloned.1.call-done, bf16[1,64,2048]{2,1,0:T(8,128)(2,1)} %convert_element_type.19), kind=kOutput, calls=%fused_computation.5 | convolution fusion | flops 537526272 | bytes 8912896 | tf_op jit(solution)/shard_map/dot_general | solution.py:39
  297.9 0.0 all-gather.4.cloned.1.call-update
  297.9 92.5 %all-gather.4.cloned.1.call-done = bf16[2048,2048]{1,0:T(8,128)(2,1)} async-done(((bf16[64,2048]{1,0:T(8,128)(2,1)}), bf16[2048,2048]{1,0:T(8,128)(2,1)}) %all-gather.4.cloned.1.call-update) | async-done | bytes 8388624 | tf_op jit(solution)/shard_map/all_gather | solution.py:56
  390.4 9.9 %multiply_convert_fusion = bf16[2048,448]{0,1:T(8,128)(2,1)} fusion(bf16[2048,448]{0,1:T(8,128)(2,1)S(1)} %copy-done, bf16[2048,2048]{1,0:T(8,128)(2,1)} %all-gather.4.cloned.1.call-done), kind=kOutput, calls=%fused_computation.2 | convolution fusion | flops 3762683904 | bytes 12058624 | tf_op jit(solution)/shard_map/dot_general | solution.py:55
  (1 shorter events, 0.0 us)
Async XLA Ops:
  6.5 44.5 %reduce-scatter.5.cloned.1.call-start = ((), (), s32[]{:S(2)}) async-start(), calls=%async_computation.4 | async-start | bytes 25165824 | tf_op jit(solution)/shard_map/reduce_scatter | solution.py:23
  19.5 115.8 %reduce-scatter.7.cloned.1.call-start = ((), (), s32[]{:S(2)}) async-start(), calls=%async_computation.5 | async-start | bytes 10485760 | tf_op jit(solution)/shard_map/reduce_scatter | solution.py:23
  51.0 120.5 %reduce-scatter.9.cloned.1.call-start = ((), (), s32[]{:S(2)}) async-start(), calls=%async_computation.6 | async-start | bytes 3145728 | tf_op jit(solution)/shard_map/reduce_scatter | solution.py:23
  135.3 63.9 %reduce-scatter.11.cloned.1.call-start = ((), (), s32[]{:S(2)}) async-start(), calls=%async_computation.7 | async-start | bytes 1572864 | tf_op jit(solution)/shard_map/reduce_scatter | solution.py:23
  171.6 120.5 %all-gather.6.cloned.1.call-start = ((), (), s32[]{:S(2)}) async-start(), calls=%async_computation.9 | async-start | bytes 8650752 | tf_op jit(solution)/shard_map/all_gather | solution.py:53
  201.0 189.4 %copy-start = (bf16[2048,448]{0,1:T(8,128)(2,1)S(1)}, bf16[2048,448]{0,1:T(8,128)(2,1)}, u32[]{:S(2)}) copy-start(bf16[2048,448]{0,1:T(8,128)(2,1)} %param.1) | copy-start | bytes 5505028
  201.1 189.3 %all-gather.4.cloned.1.call-start = ((), (), s32[]{:S(2)}) async-start(), calls=%async_computation.8 | async-start | bytes 8650752 | tf_op jit(solution)/shard_map/all_gather | solution.py:56
Sparse Core Ops, SparseCore 0:
  19.6 31.3 reduce-scatter.4
  53.5 81.7 reduce-scatter.6
  137.7 33.8 reduce-scatter.8
  173.8 25.4 reduce-scatter.10
  201.2 90.9 all-gather.5
  298.0 92.3 all-gather.3
where the time goes:
time: 407 us
  waiting for transfers between devices  363 us (89%)
  matrix products  22.4 us (6%)
  between operations  13.5 us (3%)
  local copies, waits for them, and re-layouts  6.26 us (2%)
    reduce_scatter x4, waiting for transfers between devices, reduced_to_own(): tiles = lax.psum_scatter(tiles, axes[k], scatter_dimension=0, tiled=True)  179 us
    all_gather x1, waiting for transfers between devices, body(): lax.all_gather(poly, ROW_COL_DEP, axis=0, tiled=True)  92.5 us
    all_gather x1, waiting for transfers between devices, body(): lax.all_gather(gram_half, ROW_COL_DEP, axis=0, tiled=True)  91 us
    dot_general x1, matrix products, body(): jnp.dot(lax.all_gather(poly, ROW_COL_DEP, axis=0, tiled=True), iterate, p...  9.94 us
  transfers between devices with their start and end apart: 6, of which 6 were waited for; matrix products, arithmetic and copies ran while one was open for 0% of the time, Pallas kernels for 0%

commit v1 on v0

v1 whole, which is shorter than its diff:
```python
import functools
import math

import jax
import jax.numpy as jnp
from jax import lax
from jax.experimental import pallas as pl
from jax.experimental.pallas import tpu as pltpu
from jax.sharding import PartitionSpec as P

FF = 14336
MESH = pl.DeviceIdType.MESH
BF16 = jnp.bfloat16
F32 = jnp.float32

coef_a = 3.4445
coef_b = -4.775
coef_c = 2.0315

STRIP = 128
MAIN = 256
EXTRA = 16
PIECE = MAIN + EXTRA
HALF = 144
OFFS = (2, 1, 3, 0)
UP = (0, 2)
DOWN = (1, 3)


def nt(a, b):
    return lax.dot_general(a, b, (((1,), (1,)), ((), ())), preferred_element_type=F32)


def kernel(cols, x_hbm, o_hbm, xt, x2, cf, s1, rr1, rn1, r1, s2, rr2, rn2, gs, g, yf, yb, ob, ssem, rsem, lsem):
    m, r, c, d = (lax.axis_index(a) for a in ("mat", "row", "col", "dep"))
    z = r // 2
    y = lax.rem(r, 2) * 2 + d
    depth = xt.shape[0]

    def mod4(v):
        return lax.rem(v, 4)

    def dev(yy, zz, cc):
        return (m, zz * 2 + yy // 2, cc, lax.rem(yy, 2))

    y_up, y_down = dev(mod4(y + 1), z, c), dev(mod4(y + 3), z, c)
    z_up, z_down = dev(y, mod4(z + 1), c), dev(y, mod4(z + 3), c)
    mate = dev(y, z, 1 - c)
    pos = ((y, z), (z, y))
    links = (((y_up, y_down), (z_up, z_down)), ((z_up, z_down), (y_up, y_down)))

    count = [0]
    started = []

    def send(src, dst, to):
        k = count[0]
        count[0] += 1
        copy = pltpu.make_async_remote_copy(
            src_ref=src, dst_ref=dst, send_sem=ssem.at[k], recv_sem=rsem.at[k], device_id=to, device_id_type=MESH
        )
        copy.start()
        started.append(copy)
        return copy

    load = pltpu.make_async_copy(x_hbm, xt.at[pl.ds(0, cols)], lsem.at[0])
    load.start()
    barrier = pltpu.get_barrier_semaphore()
    for other in (y_up, y_down, z_up, z_down, mate):
        pl.semaphore_signal(barrier, inc=1, device_id=other, device_id_type=MESH)
    if depth > cols:
        xt[cols:, :] = jnp.zeros((depth - cols, xt.shape[1]), BF16)
    load.wait()
    pl.semaphore_wait(barrier, 5)

    n_rows = xt.shape[1]
    half_rows = n_rows // 2
    swaps = []
    for part in range(2):
        for s in range(8):
            row = part * half_rows + s * STRIP
            there = pl.multiple_of(lax.rem(row + half_rows * c, n_rows), STRIP)
            x2[row : row + STRIP, 0:depth] = xt[:, pl.ds(there, STRIP)].T
        swaps.append(
            send(
                x2.at[pl.ds(part * half_rows, half_rows), pl.ds(0, depth)],
                x2.at[pl.ds((1 - part) * half_rows, half_rows), pl.ds(depth, depth)],
                mate,
            )
        )
    for copy in swaps:
        copy.wait_recv()

    def gram(h, j):
        u = 4 * h + mod4(pos[h][0] + OFFS[j])
        top = pl.multiple_of(u * STRIP, STRIP)
        main = nt(x2[pl.ds(top, 8 * STRIP), :], x2[pl.ds(top, STRIP), :])
        for t in range(4):
            cf[h, j, t, 0:MAIN] = main[t * MAIN : (t + 1) * MAIN]
        left = pl.multiple_of(u * STRIP + half_rows * (1 - c) + 64 * c, 64)
        right = pl.multiple_of(u * STRIP + half_rows * c, STRIP)
        extra = nt(x2[pl.ds(left, 64), :], x2[pl.ds(right, STRIP), :])
        for t in range(4):
            cf[h, j, t, MAIN:PIECE] = extra[t * EXTRA : (t + 1) * EXTRA]

    def mine(h, j, k):
        return cf[h, j, mod4(pos[h][1] + OFFS[k])]

    relay = {}
    near = {}
    for h in range(2):
        up, down = links[h][0]
        gram(h, 0)
        for i in range(2):
            for k, to, w in ((UP[i], up, 0), (DOWN[i], down, 1)):
                s1[h, 0, k] = mine(h, 0, k).astype(BF16)
                relay[h, w, k] = send(s1.at[h, 0, k], rr1.at[h, w, i], to)
    for h in range(2):
        up, down = links[h][0]
        for j, to, w, plain in ((1, up, 0, DOWN), (2, down, 1, UP)):
            gram(h, j)
            for k in plain:
                s1[h, j, k] = mine(h, j, k).astype(BF16)
                near[h, w, k] = send(s1.at[h, j, k], rn1.at[h, w, k], to)
    for i in range(2):
        for h in range(2):
            up, down = links[h][0]
            for j, to, w, k in ((1, up, 0, UP[i]), (2, down, 1, DOWN[i])):
                relay[h, w, k].wait_recv()
                s1[h, j, k] = (mine(h, j, k) + rr1[h, w, i].astype(F32)).astype(BF16)
                near[h, w, k] = send(s1.at[h, j, k], rn1.at[h, w, k], to)
    for h in range(2):
        gram(h, 3)

    relay2 = {}
    near2 = {}
    a_rows, b_rows = pl.ds(0, HALF), pl.ds(HALF, PIECE - HALF)
    for k in range(3):
        for h in range(2):
            up, down = links[h][1]
            near[h, 0, k].wait_recv()
            near[h, 1, k].wait_recv()
            total = mine(h, 3, k) + rn1[h, 0, k].astype(F32) + rn1[h, 1, k].astype(F32)
            if k == 0:
                s2[h, 0] = total.astype(BF16)
                relay2[h, 0] = send(s2.at[h, 0, a_rows], rr2.at[h, 0, a_rows], up)
                relay2[h, 1] = send(s2.at[h, 0, b_rows], rr2.at[h, 1, b_rows], down)
            elif k == 1:
                r1[h, 0] = total[:HALF]
                s2[h, 1, HALF:] = total[HALF:].astype(BF16)
                near2[h, 0, 1] = send(s2.at[h, 1, b_rows], rn2.at[h, 0, b_rows], up)
            else:
                r1[h, 1, : PIECE - HALF] = total[HALF:]
                s2[h, 2, :HALF] = total[:HALF].astype(BF16)
                near2[h, 1, 0] = send(s2.at[h, 2, a_rows], rn2.at[h, 1, a_rows], down)
    for h in range(2):
        up, down = links[h][1]
        relay2[h, 0].wait_recv()
        s2[h, 1, :HALF] = (r1[h, 0] + rr2[h, 0, :HALF].astype(F32)).astype(BF16)
        near2[h, 0, 0] = send(s2.at[h, 1, a_rows], rn2.at[h, 0, a_rows], up)
        relay2[h, 1].wait_recv()
        s2[h, 2, HALF:] = (r1[h, 1, : PIECE - HALF] + rr2[h, 1, HALF:].astype(F32)).astype(BF16)
        near2[h, 1, 1] = send(s2.at[h, 2, b_rows], rn2.at[h, 1, b_rows], down)
    for h in range(2):
        near[h, 0, 3].wait_recv()
        near[h, 1, 3].wait_recv()
        r1[h, 2] = (mine(h, 3, 3) + rn1[h, 0, 3].astype(F32) + rn1[h, 1, 3].astype(F32))[:HALF]
        r1[h, 3, : PIECE - HALF] = (mine(h, 3, 3) + rn1[h, 0, 3].astype(F32) + rn1[h, 1, 3].astype(F32))[HALF:]

    def slot(h, dp, dq, rows=None):
        p, q = mod4(pos[h][0] + dp), mod4(pos[h][1] + dq)
        ref = gs.at[c, h, p, q]
        return ref if rows is None else ref.at[rows]

    def push(h, dp, dq, to, rows=None):
        return send(slot(h, dp, dq, rows), slot(h, dp, dq, rows), to)

    def place(cc, h, dp, dq):
        p, q = mod4(pos[h][0] + dp), mod4(pos[h][1] + dq)
        uu = 4 * h + p
        u = 8 * cc + uu
        col = pl.multiple_of(u * STRIP, STRIP)
        for i in range(2):
            v = lax.rem(u + 2 * q + i, 16)
            row = pl.multiple_of(v * STRIP, STRIP)
            block = gs[cc, h, p, q, i * STRIP : (i + 1) * STRIP]
            g[pl.ds(row, STRIP), pl.ds(col, STRIP)] = block
            g[pl.ds(col, STRIP), pl.ds(row, STRIP)] = block.T
        row = pl.multiple_of((uu + 8) * STRIP + 64 * cc + EXTRA * q, EXTRA)
        ecol = pl.multiple_of(uu * STRIP, STRIP)
        g[pl.ds(row, EXTRA), pl.ds(ecol, STRIP)] = gs[cc, h, p, q, MAIN:PIECE]

    first, second, half, hop, cross = {}, {}, {}, {}, {}
    for h in range(2):
        (up1, down1), (up2, down2) = links[h]
        for w in range(2):
            near2[h, w, 0].wait_recv()
            near2[h, w, 1].wait_recv()
        here = rn2[h, 0].astype(F32) + rn2[h, 1].astype(F32)
        p, q = pos[h]
        gs[c, h, p, q, :HALF] = (r1[h, 2] + here[:HALF]).astype(BF16)
        gs[c, h, p, q, HALF:] = (r1[h, 3, : PIECE - HALF] + here[HALF:]).astype(BF16)
        first[h, 0] = push(h, 0, 0, up2)
        first[h, 1] = push(h, 0, 0, down2)
        second[h, 0, 0] = push(h, 0, 0, up1)
        second[h, 1, 0] = push(h, 0, 0, down1)
        cross[h, 0, 0] = push(h, 0, 0, mate)
    for h in range(2):
        (up1, down1), (up2, down2) = links[h]
        for w, dq, to, rows in ((0, 3, up2, a_rows), (1, 1, down2, b_rows)):
            first[h, w].wait_recv()
            half[h, w] = push(h, 0, dq, to, rows)
            second[h, 0, dq] = push(h, 0, dq, up1)
            second[h, 1, dq] = push(h, 0, dq, down1)
            cross[h, 0, dq] = push(h, 0, dq, mate)

    def arrive(h, dq):
        (up1, down1), _ = links[h]
        for w, dp, to, ahead in ((0, 3, up1, (0, 1)), (1, 1, down1, (3, 2))):
            second[h, w, dq].wait_recv()
            if dq in ahead:
                hop[h, dq] = push(h, dp, dq, to)
            cross[h, dp, dq] = push(h, dp, dq, mate)

    for h in range(2):
        arrive(h, 0)
    for h in range(2):
        (up1, down1), _ = links[h]
        half[h, 0].wait_recv()
        half[h, 1].wait_recv()
        second[h, 0, 2] = push(h, 0, 2, up1)
        second[h, 1, 2] = push(h, 0, 2, down1)
        cross[h, 0, 2] = push(h, 0, 2, mate)
    for dq in (1, 3):
        for h in range(2):
            arrive(h, dq)
    for h in range(2):
        for dq in (0, 1, 3):
            place(c, h, 0, dq)
    for h in range(2):
        arrive(h, 2)
    for h in range(2):
        for dp, dq in ((0, 2), (3, 0), (1, 0), (3, 1), (1, 1), (3, 3), (1, 3), (3, 2), (1, 2)):
            place(c, h, dp, dq)
    for h in range(2):
        for dq in (0, 1, 3, 2):
            hop[h, dq].wait_recv()
            cross[h, 2, dq] = push(h, 2, dq, mate)
    for h in range(2):
        for dp, dq in ((0, 0), (0, 3), (0, 1), (0, 2), (3, 0), (1, 0), (3, 1), (1, 1), (3, 3), (1, 3), (3, 2), (1, 2)):
            cross[h, dp, dq].wait_recv()
            place(1 - c, h, dp, dq)
    for h in range(2):
        for dq in (0, 1, 3, 2):
            place(c, h, 2, dq)
    for h in range(2):
        for dq in (0, 1, 3, 2):
            cross[h, 2, dq].wait_recv()
            place(1 - c, h, 2, dq)
    for uu in range(8):
        a, b = slice(uu * STRIP, (uu + 1) * STRIP), slice((uu + 8) * STRIP, (uu + 9) * STRIP)
        g[a, b] = g[b, a].T

    wide = 256
    x_t = xt[0:cols, :]

    @pl.loop(0, n_rows // wide)
    def _(n):
        at = pl.ds(pl.multiple_of(n * wide, wide), wide)
        part = jnp.dot(xt[0:cols, :], g[:, at], preferred_element_type=F32)
        yf[:, at] = part
        yb[:, at] = part.astype(BF16)

    scale = math.sqrt(FF)

    @pl.loop(0, n_rows // wide)
    def _(n):
        at = pl.ds(pl.multiple_of(n * wide, wide), wide)
        part = jnp.dot(yb[...], g[:, at], preferred_element_type=F32)
        updated = coef_a * xt[0:cols, at].astype(F32) + (coef_b * yf[:, at] + coef_c * part)
        ob[:, at] = (scale * updated).astype(BF16)
        pltpu.make_async_copy(ob.at[:, at], o_hbm.at[:, at], lsem.at[1 + n]).start()

    @pl.loop(0, n_rows // wide)
    def _(n):
        at = pl.ds(pl.multiple_of(n * wide, wide), wide)
        pltpu.make_async_copy(ob.at[:, at], o_hbm.at[:, at], lsem.at[1 + n]).wait()

    for copy in started:
        copy.wait_send()


def body(iterate):
    x = iterate.T
    cols, rows = x.shape
    depth = -(-cols // 128) * 128
    copies = 2 + 2 * (12 + 8 + 4 + 12 + 16)
    out = pl.pallas_call(
        functools.partial(kernel, cols),
        out_shape=jax.ShapeDtypeStruct((cols, rows), BF16),
        in_specs=[pl.BlockSpec(memory_space=pl.ANY)],
        out_specs=pl.BlockSpec(memory_space=pl.ANY),
        scratch_shapes=[
            pltpu.VMEM((depth, rows), BF16),
            pltpu.VMEM((rows, 2 * depth), BF16),
            pltpu.VMEM((2, 4, 4, PIECE, STRIP), F32),
            pltpu.VMEM((2, 3, 4, PIECE, STRIP), BF16),
            pltpu.VMEM((2, 2, 2, PIECE, STRIP), BF16),
            pltpu.VMEM((2, 2, 4, PIECE, STRIP), BF16),
            pltpu.VMEM((2, 4, HALF, STRIP), F32),
            pltpu.VMEM((2, 3, PIECE, STRIP), BF16),
            pltpu.VMEM((2, 2, PIECE, STRIP), BF16),
            pltpu.VMEM((2, 2, PIECE, STRIP), BF16),
            pltpu.VMEM((2, 2, 4, 4, PIECE, STRIP), BF16),
            pltpu.VMEM((rows, rows), BF16),
            pltpu.VMEM((cols, rows), F32),
            pltpu.VMEM((cols, rows), BF16),
            pltpu.VMEM((cols, rows), BF16),
            pltpu.SemaphoreType.DMA((copies,)),
            pltpu.SemaphoreType.DMA((copies,)),
            pltpu.SemaphoreType.DMA((1 + rows // 256,)),
        ],
        compiler_params=pltpu.CompilerParams(
            collective_id=0, has_side_effects=True, vmem_limit_bytes=60 * 1024 * 1024
        ),
    )(x)
    return out.T


def solution(mesh):
    spec = P("mat", ("row", "col", "dep"))
    return jax.shard_map(body, mesh=mesh, in_specs=(spec,), out_specs=spec, check_vma=False)
```

time: 407 us -> 66.4 us (0.16)
  waiting for transfers between devices: 363 us -> 0 us
  Pallas kernels: 0 us -> 62.4 us
  matrix products: 22.4 us -> 0 us
  between operations: 13.5 us -> 0.01 us
    all_gather x2 -> x0, waiting for transfers between devices: 184 us -> none  [the longest x1 92.5 us: body(): lax.all_gather(poly, ROW_COL_DEP, axis=0, tiled=True)]
    reduce_scatter x4 -> x0, waiting for transfers between devices: 179 us -> none  [reduced_to_own(): tiles = lax.psum_scatter(tiles, axes[k], scatter_dimension=0, tiled=True)]
    pallas_call x0 -> x1, Pallas kernels: none -> 62.4 us  [body(): pl.pallas_call(functools.partial(kernel, cols), out_shape=jax.ShapeDtypeS...]
    dot_general x3 -> x0, matrix products: 22.4 us -> none  [the longest x1 9.94 us: body(): jnp.dot(lax.all_gather(poly, ROW_COL_DEP, axis=0, tiled=True), iterate, p...]
    another operation x1 -> x0, local copies, waits for them, and re-layouts: 6.25 us -> none  [reduced_to_own(): tiles = tiles.reshape(*(lax.axis_size(a) for a in axes), *inside)]
  transfers between devices with their start and end apart: 6 -> 0, of which waited for: 6 -> 0; matrix products, arithmetic and copies ran while one was open for 0% -> 0% of each run, Pallas kernels for 0% -> 0%
where the time goes in v1:
time: 66.4 us; the launch traced here: 65.4 us
  Pallas kernels  62.4 us (94%)
  local copies, waits for them, and re-layouts  2.94 us (4%)
    pallas_call x1, Pallas kernels, body(): pl.pallas_call(functools.partial(kernel, cols), out_shape=jax.ShapeDtypeS...  62.4 us
    unnamed x1, local copies, waits for them, and re-layouts  2.94 us

profile of v1, /device:TPU:1, one launch (start us, length us, event | category | flops | bytes accessed | tf_op | source)
XLA Modules:
  0.0 65.4 jit_solution(9271794275118154051)
XLA Ops:
  0.0 62.4 %shard_map.17 = bf16[448,2048]{1,0:T(8,128)(2,1)} custom-call(bf16[448,2048]{1,0:T(8,128)(2,1)} %bitcast.3), custom_call_target="tpu_custom_call" | custom-call | tf_op jit(solution)/shard_map/pallas_call | solution.py:297
  62.4 2.9 %copy.3 = bf16[2048,448]{0,1:T(8,128)(2,1)} copy(bf16[2048,448]{0,1:T(8,128)(2,1)} %bitcast.2) | data formatting | bytes 3670016

commit v2 on v0

v2 whole, which is shorter than its diff:
```python
import functools
import math

import jax
import jax.numpy as jnp
from jax import lax
from jax.experimental import pallas as pl
from jax.experimental.pallas import tpu as pltpu
from jax.sharding import PartitionSpec as P

FF = 14336
MESH = pl.DeviceIdType.MESH
BF16 = jnp.bfloat16
F32 = jnp.float32

coef_a = 3.4445
coef_b = -4.775
coef_c = 2.0315

STRIP = 128
EXTRA = 16
ROWS_OF = (STRIP, STRIP + EXTRA)
OFFS = (2, 3, 1, 0)
PAIR = 2 * STRIP


def nt(a, b):
    return lax.dot_general(a, b, (((1,), (1,)), ((), ())), preferred_element_type=F32)


def kernel(cols, x_hbm, o_hbm, xt, x2, cf0, cf1, s10, s11, rr10, rr11, rn10, rn11, r10, r11, s20, s21, rn20, rn21,
           gs0, gs1, g, yf, yb, ob, ssem, rsem, lsem):
    cf, s1, rr1, rn1, r1 = (cf0, cf1), (s10, s11), (rr10, rr11), (rn10, rn11), (r10, r11)
    s2, rn2, gs = (s20, s21), (rn20, rn21), (gs0, gs1)
    m, r, c, d = (lax.axis_index(a) for a in ("mat", "row", "col", "dep"))
    z = r // 2
    y = lax.rem(r, 2) * 2 + d
    depth, n_rows = xt.shape
    half_rows = n_rows // 2

    def mod4(v):
        return lax.rem(v, 4)

    def dev(yy, zz, cc):
        return (m, zz * 2 + yy // 2, cc, lax.rem(yy, 2))

    y_up, y_down = dev(mod4(y + 1), z, c), dev(mod4(y + 3), z, c)
    z_up, z_down = dev(y, mod4(z + 1), c), dev(y, mod4(z + 3), c)
    y_far, z_far = dev(mod4(y + 2), z, c), dev(y, mod4(z + 2), c)
    mate = dev(y, z, 1 - c)
    pos = ((y, z), (z, y))
    links = (((y_up, y_down), (z_up, z_down)), ((z_up, z_down), (y_up, y_down)))
    fars = ((y_far, z_far), (z_far, y_far))

    count = [0]
    started = []

    def send(src, dst, to):
        k = count[0]
        count[0] += 1
        copy = pltpu.make_async_remote_copy(
            src_ref=src, dst_ref=dst, send_sem=ssem.at[k], recv_sem=rsem.at[k], device_id=to, device_id_type=MESH
        )
        copy.start()
        started.append(copy)
        return copy

    loads = []
    for part in (1, 0):
        there = pl.ds(pl.multiple_of(lax.rem(part + c, 2) * half_rows, half_rows), half_rows)
        copy = pltpu.make_async_copy(x_hbm.at[:, there], xt.at[pl.ds(0, cols), there], lsem.at[part])
        copy.start()
        loads.append(copy)
    barrier = pltpu.get_barrier_semaphore()
    for other in (mate, y_up, y_down, z_up, z_down, y_far, z_far):
        pl.semaphore_signal(barrier, inc=1, device_id=other, device_id_type=MESH)
    if depth > cols:
        xt[cols:, :] = jnp.zeros((depth - cols, n_rows), BF16)
    swaps = {}
    for part, load in zip((1, 0), loads):
        load.wait()
        for s in range(half_rows // STRIP):
            row = part * half_rows + s * STRIP
            there = pl.multiple_of(lax.rem(row + half_rows * c, n_rows), STRIP)
            x2[row : row + STRIP, 0:depth] = xt[:, pl.ds(there, STRIP)].T
        if part == 1:
            pl.semaphore_wait(barrier, 7)
        swaps[part] = send(
            x2.at[pl.ds(part * half_rows, half_rows), pl.ds(0, depth)],
            x2.at[pl.ds((1 - part) * half_rows, half_rows), pl.ds(depth, depth)],
            mate,
        )

    def gram(e, h, which, part):
        pair = mod4(pos[h][0] + 2) // 2
        pair = pair if which == 0 else 1 - pair
        top = pl.multiple_of((4 * h + 2 * pair) * STRIP, PAIR)
        lanes = slice(part * depth, (part + 1) * depth)
        if e == 0:
            out = nt(x2[pl.ds(top, 5 * STRIP), lanes], x2[pl.ds(top, PAIR), lanes])
        else:
            out = nt(x2[pl.ds(top + 4 * STRIP, 6 * STRIP), lanes], x2[pl.ds(top, PAIR), lanes])
        for i in range(2):
            own = slice(i * STRIP, (i + 1) * STRIP)
            rows = [out[(i + q) * STRIP : (i + q + 1) * STRIP, own] for q in range(4)]
            if e == 1:
                block = out[(i + 4) * STRIP : (i + 5) * STRIP, own]
                extra = jnp.where(c == 0, block[:64], block.T[64:])
            for q in range(4):
                at = cf[e].at[h, 2 * pair + i, q]
                at[:STRIP] = rows[q] if part == 0 else at[:STRIP] + rows[q]
                if e == 1:
                    more = extra[q * EXTRA : (q + 1) * EXTRA]
                    at[STRIP:] = more if part == 0 else at[STRIP:] + more

    def mine(e, h, j, k):
        return cf[e][h, mod4(pos[h][0] + j), mod4(pos[h][1] + OFFS[k])]

    up_ks, down_ks = pl.ds(0, 2), pl.ds(2, 2)
    relay, near = {}, {}

    def relay_out(e, h):
        up, down = links[h][0]
        for k in range(4):
            s1[e][h, 0, k] = mine(e, h, 2, k).astype(BF16)
            if k == 1:
                relay[e, h, 0] = send(s1[e].at[h, 0, up_ks], rr1[e].at[h, 0], up)
        relay[e, h, 1] = send(s1[e].at[h, 0, down_ks], rr1[e].at[h, 1], down)

    def plain_out(e, h):
        up, down = links[h][0]
        for k in (2, 3):
            s1[e][h, 1, k] = mine(e, h, 1, k).astype(BF16)
        near[e, h, 0, 1] = send(s1[e].at[h, 1, down_ks], rn1[e].at[h, 0, down_ks], up)
        for k in (0, 1):
            s1[e][h, 2, k] = mine(e, h, 3, k).astype(BF16)
        near[e, h, 1, 0] = send(s1[e].at[h, 2, up_ks], rn1[e].at[h, 1, up_ks], down)

    def merged_out(e, h):
        up, down = links[h][0]
        relay[e, h, 0].wait_recv()
        for k in (0, 1):
            s1[e][h, 1, k] = (mine(e, h, 1, k) + rr1[e][h, 0, k].astype(F32)).astype(BF16)
        near[e, h, 0, 0] = send(s1[e].at[h, 1, up_ks], rn1[e].at[h, 0, up_ks], up)
        relay[e, h, 1].wait_recv()
        for k in (2, 3):
            s1[e][h, 2, k] = (mine(e, h, 3, k) + rr1[e][h, 1, k - 2].astype(F32)).astype(BF16)
        near[e, h, 1, 1] = send(s1[e].at[h, 2, down_ks], rn1[e].at[h, 1, down_ks], down)

    near2 = {}

    def ring2_first(e, h):
        up, down = links[h][1]

        def total(k):
            return mine(e, h, 0, k) + (rn1[e][h, 0, k].astype(F32) + rn1[e][h, 1, k].astype(F32))

        def out(k, w, to):
            s2[e][h, w] = total(k).astype(BF16)
            near2[e, h, w] = send(s2[e].at[h, w], rn2[e].at[h, w], to)

        near[e, h, 0, 1].wait_recv()
        near[e, h, 1, 0].wait_recv()
        near[e, h, 0, 0].wait_recv()
        out(0, 0, fars[h][1])
        out(1, 1, down)
        near[e, h, 1, 1].wait_recv()
        out(2, 2, up)
        r1[e][h] = total(3)

    first, second, hop, cross = {}, {}, {}, {}

    def push(e, h, dp, dq, to):
        ref = gs[e].at[c, h, mod4(pos[h][0] + dp), mod4(pos[h][1] + dq)]
        return send(ref, ref, to)

    def push_strip(e, h, dp):
        ref = gs[e].at[c, h, mod4(pos[h][0] + dp)]
        cross[e, h, dp] = send(ref, ref, mate)

    def push_near(e, h, dq):
        up, down = links[h][0]
        second[e, h, 0, dq] = push(e, h, 0, dq, up)
        second[e, h, 1, dq] = push(e, h, 0, dq, down)

    def ring2_own(e, h):
        up, down = links[h][1]
        for w in (1, 2, 0):
            near2[e, h, w].wait_recv()
        p, q = pos[h]
        others = rn2[e][h, 0].astype(F32) + (rn2[e][h, 1].astype(F32) + rn2[e][h, 2].astype(F32))
        gs[e][c, h, p, q] = (r1[e][h] + others).astype(BF16)
        first[e, h, 2] = push(e, h, 0, 0, fars[h][1])
        first[e, h, 3] = push(e, h, 0, 0, up)
        first[e, h, 1] = push(e, h, 0, 0, down)
        push_near(e, h, 0)

    def gather_sides(e, h):
        for dq in (3, 1):
            first[e, h, dq].wait_recv()
            push_near(e, h, dq)

    def gather_far(e, h):
        first[e, h, 2].wait_recv()
        hop[e, h, 2] = push(e, h, 0, 2, fars[h][0])
        push_near(e, h, 2)
        push_strip(e, h, 0)

    def arrive(e, h, dq):
        up, down = links[h][0]
        for w, dp, to, ahead in ((0, 3, up, (0, 1) if h == 0 else (1,)), (1, 1, down, (3,) if h == 0 else (0, 3))):
            second[e, h, w, dq].wait_recv()
            if dq in ahead:
                hop[e, h, dq] = push(e, h, dp, dq, to)
            if dq == 2:
                push_strip(e, h, dp)

    def hops(e, h):
        for dq in (0, 1, 3, 2):
            hop[e, h, dq].wait_recv()
        push_strip(e, h, 2)

    def place(e, cc, h, dp):
        p = mod4(pos[h][0] + dp)
        uu = 4 * h + p
        u = 8 * cc + uu
        col = pl.multiple_of(u * STRIP, STRIP)
        for q in range(4):
            row = pl.multiple_of(lax.rem(u + 4 * e + q, 16) * STRIP, STRIP)
            block = gs[e][cc, h, p, q, :STRIP]
            g[pl.ds(row, STRIP), pl.ds(col, STRIP)] = block
            g[pl.ds(col, STRIP), pl.ds(row, STRIP)] = block.T
            if e == 1:
                row = pl.multiple_of((uu + 8) * STRIP + 64 * cc + EXTRA * q, EXTRA)
                ecol = pl.multiple_of(uu * STRIP, STRIP)
                g[pl.ds(row, EXTRA), pl.ds(ecol, STRIP)] = gs[1][cc, h, p, q, STRIP:]

    def place_mate(e, h, dp):
        cross[e, h, dp].wait_recv()
        place(e, 1 - c, h, dp)

    def both(f, *args):
        for h in range(2):
            f(args[0], h, *args[1:])

    def times_g(left, n, pairs):
        runs = []
        for k in pairs:
            k %= n_rows // PAIR
            if runs and runs[-1][1] == k:
                runs[-1][1] = k + 1
            else:
                runs.append([k, k + 1])
        return sum(
            jnp.dot(left[0:cols, lo * PAIR : hi * PAIR], g[lo * PAIR : hi * PAIR, n * PAIR : (n + 1) * PAIR], preferred_element_type=F32)
            for lo, hi in runs
        )

    n_pairs = n_rows // PAIR
    for e in range(2):
        for which in range(2):
            for h in range(2):
                gram(e, h, which, 0)
    for h in range(2):
        swaps[1 - h].wait_recv()
        gram(0, h, 0, 1)
        relay_out(0, h)
    for h in range(2):
        gram(0, h, 1, 1)
        plain_out(0, h)
    for h in range(2):
        gram(1, h, 0, 1)
        relay_out(1, h)
    both(merged_out, 0)
    for h in range(2):
        gram(1, h, 1, 1)
        plain_out(1, h)
    both(merged_out, 1)
    both(ring2_first, 0)
    both(ring2_own, 0)
    both(ring2_first, 1)
    both(gather_sides, 0)
    both(arrive, 0, 0)
    both(gather_far, 0)
    both(ring2_own, 1)
    both(arrive, 0, 1)
    both(arrive, 0, 3)
    both(gather_sides, 1)
    both(arrive, 0, 2)
    both(arrive, 1, 0)
    both(gather_far, 1)
    for h in range(2):
        for dp in (0, 3, 1):
            place(0, c, h, dp)
    both(hops, 0)
    both(arrive, 1, 1)
    both(arrive, 1, 3)
    for dp in (0, 3, 1):
        both(place_mate, 0, dp)
    for h in range(2):
        place(0, c, h, 2)
    both(arrive, 1, 2)
    both(place_mate, 0, 2)
    for n in range(n_pairs):
        yf[:, n * PAIR : (n + 1) * PAIR] = times_g(xt, n, range(n - 1, n + 2))
    for h in range(2):
        for dp in (0, 3, 1):
            place(1, c, h, dp)
    both(hops, 1)
    for dp in (0, 3, 1):
        both(place_mate, 1, dp)
    for h in range(2):
        place(1, c, h, 2)
    both(place_mate, 1, 2)
    for uu in range(8):
        a, b = slice(uu * STRIP, (uu + 1) * STRIP), slice((uu + 8) * STRIP, (uu + 9) * STRIP)
        g[a, b] = g[b, a].T
    for n in range(n_pairs):
        at = slice(n * PAIR, (n + 1) * PAIR)
        part = yf[:, at] + times_g(xt, n, range(n + 2, n + n_pairs - 1))
        yf[:, at] = part
        yb[:, at] = part.astype(BF16)
    scale = math.sqrt(FF)
    outs = []
    for n in range(n_pairs):
        at = slice(n * PAIR, (n + 1) * PAIR)
        part = times_g(yb, n, range(n_pairs))
        updated = coef_a * xt[0:cols, at].astype(F32) + (coef_b * yf[:, at] + coef_c * part)
        ob[:, at] = (scale * updated).astype(BF16)
        lanes = pl.ds(n * PAIR, PAIR)
        copy = pltpu.make_async_copy(ob.at[:, lanes], o_hbm.at[:, lanes], lsem.at[2 + n])
        copy.start()
        outs.append(copy)
    for copy in outs:
        copy.wait()
    for copy in started:
        copy.wait_send()


def body(iterate):
    x = iterate.T
    cols, rows = x.shape
    depth = -(-cols // 128) * 128
    copies = 2 + 4 * (6 + 3 + 3 + 12 + 4)

    def each(*dims, dtype=BF16):
        return [pltpu.VMEM((*dims, n, STRIP), dtype) for n in ROWS_OF]

    out = pl.pallas_call(
        functools.partial(kernel, cols),
        out_shape=jax.ShapeDtypeStruct((cols, rows), BF16),
        in_specs=[pl.BlockSpec(memory_space=pl.ANY)],
        out_specs=pl.BlockSpec(memory_space=pl.ANY),
        scratch_shapes=[
            pltpu.VMEM((depth, rows), BF16),
            pltpu.VMEM((rows, 2 * depth), BF16),
            *each(2, 4, 4, dtype=F32),
            *each(2, 3, 4),
            *each(2, 2, 2),
            *each(2, 2, 4),
            *each(2, dtype=F32),
            *each(2, 3),
            *each(2, 3),
            *each(2, 2, 4, 4),
            pltpu.VMEM((rows, rows), BF16),
            pltpu.VMEM((cols, rows), F32),
            pltpu.VMEM((cols, rows), BF16),
            pltpu.VMEM((cols, rows), BF16),
            pltpu.SemaphoreType.DMA((copies,)),
            pltpu.SemaphoreType.DMA((copies,)),
            pltpu.SemaphoreType.DMA((2 + rows // PAIR,)),
        ],
        compiler_params=pltpu.CompilerParams(
            collective_id=0, has_side_effects=True, vmem_limit_bytes=60 * 1024 * 1024
        ),
    )(x)
    return out.T


def solution(mesh):
    spec = P("mat", ("row", "col", "dep"))
    return jax.shard_map(body, mesh=mesh, in_specs=(spec,), out_specs=spec, check_vma=False)
```

time: 407 us -> 58.5 us (0.14)
  waiting for transfers between devices: 363 us -> 0 us
  Pallas kernels: 0 us -> 55.4 us
  matrix products: 22.4 us -> 0 us
  between operations: 13.5 us -> 0.01 us
    all_gather x2 -> x0, waiting for transfers between devices: 184 us -> none  [the longest x1 92.5 us: body(): lax.all_gather(poly, ROW_COL_DEP, axis=0, tiled=True)]
    reduce_scatter x4 -> x0, waiting for transfers between devices: 179 us -> none  [reduced_to_own(): tiles = lax.psum_scatter(tiles, axes[k], scatter_dimension=0, tiled=True)]
    pallas_call x0 -> x1, Pallas kernels: none -> 55.4 us  [body(): pl.pallas_call(functools.partial(kernel, cols), out_shape=jax.ShapeDtypeS...]
    dot_general x3 -> x0, matrix products: 22.4 us -> none  [the longest x1 9.94 us: body(): jnp.dot(lax.all_gather(poly, ROW_COL_DEP, axis=0, tiled=True), iterate, p...]
    another operation x1 -> x0, local copies, waits for them, and re-layouts: 6.25 us -> none  [reduced_to_own(): tiles = tiles.reshape(*(lax.axis_size(a) for a in axes), *inside)]
  transfers between devices with their start and end apart: 6 -> 0, of which waited for: 6 -> 0; matrix products, arithmetic and copies ran while one was open for 0% -> 0% of each run, Pallas kernels for 0% -> 0%
where the time goes in v2:
time: 58.5 us; the launch traced here: 58.3 us
  Pallas kernels  55.4 us (95%)
  local copies, waits for them, and re-layouts  2.94 us (5%)
    pallas_call x1, Pallas kernels, body(): pl.pallas_call(functools.partial(kernel, cols), out_shape=jax.ShapeDtypeS...  55.4 us
    unnamed x1, local copies, waits for them, and re-layouts  2.94 us

profile of v2, /device:TPU:1, one launch (start us, length us, event | category | flops | bytes accessed | tf_op | source)
XLA Modules:
  0.0 58.3 jit_solution(12386197902418838320)
XLA Ops:
  0.0 55.4 %shard_map.17 = bf16[448,2048]{1,0:T(8,128)(2,1)} custom-call(bf16[448,2048]{1,0:T(8,128)(2,1)} %bitcast.3), custom_call_target="tpu_custom_call" | custom-call | tf_op jit(solution)/shard_map/pallas_call | solution.py:349
  55.4 2.9 %copy.3 = bf16[2048,448]{0,1:T(8,128)(2,1)} copy(bf16[2048,448]{0,1:T(8,128)(2,1)} %bitcast.2) | data formatting | bytes 3670016

commit v3 on v2

--- a/solution.py
+++ b/solution.py
@@ -28,14 +28,14 @@
     return lax.dot_general(a, b, (((1,), (1,)), ((), ())), preferred_element_type=F32)
 
 
-def kernel(cols, x_hbm, o_hbm, xt, x2, cf0, cf1, s10, s11, rr10, rr11, rn10, rn11, r10, r11, s20, s21, rn20, rn21,
-           gs0, gs1, g, yf, yb, ob, ssem, rsem, lsem):
+def kernel(depth, x_hbm, o_ref, x_ref, x2, cf0, cf1, s10, s11, rr10, rr11, rn10, rn11, r10, r11, s20, s21, rn20, rn21,
+           gs0, gs1, g, yf, yb, ssem, rsem, lsem):
     cf, s1, rr1, rn1, r1 = (cf0, cf1), (s10, s11), (rr10, rr11), (rn10, rn11), (r10, r11)
     s2, rn2, gs = (s20, s21), (rn20, rn21), (gs0, gs1)
     m, r, c, d = (lax.axis_index(a) for a in ("mat", "row", "col", "dep"))
     z = r // 2
     y = lax.rem(r, 2) * 2 + d
-    depth, n_rows = xt.shape
+    cols, n_rows = x_ref.shape
     half_rows = n_rows // 2
 
     def mod4(v):
@@ -68,28 +68,32 @@
     loads = []
     for part in (1, 0):
         there = pl.ds(pl.multiple_of(lax.rem(part + c, 2) * half_rows, half_rows), half_rows)
-        copy = pltpu.make_async_copy(x_hbm.at[:, there], xt.at[pl.ds(0, cols), there], lsem.at[part])
+        copy = pltpu.make_async_copy(x_hbm.at[:, there], x_ref.at[:, there], lsem.at[part])
         copy.start()
         loads.append(copy)
     barrier = pltpu.get_barrier_semaphore()
     for other in (mate, y_up, y_down, z_up, z_down, y_far, z_far):
         pl.semaphore_signal(barrier, inc=1, device_id=other, device_id_type=MESH)
-    if depth > cols:
-        xt[cols:, :] = jnp.zeros((depth - cols, n_rows), BF16)
-    swaps = {}
+    swaps = []
     for part, load in zip((1, 0), loads):
         load.wait()
         for s in range(half_rows // STRIP):
             row = part * half_rows + s * STRIP
             there = pl.multiple_of(lax.rem(row + half_rows * c, n_rows), STRIP)
-            x2[row : row + STRIP, 0:depth] = xt[:, pl.ds(there, STRIP)].T
+            strip = x_ref[:, pl.ds(there, STRIP)]
+            if depth > cols:
+                strip = jnp.concatenate([strip, jnp.zeros((depth - cols, STRIP), BF16)], axis=0)
+            x2[row : row + STRIP, 0:depth] = strip.T
         if part == 1:
             pl.semaphore_wait(barrier, 7)
-        swaps[part] = send(
-            x2.at[pl.ds(part * half_rows, half_rows), pl.ds(0, depth)],
-            x2.at[pl.ds((1 - part) * half_rows, half_rows), pl.ds(depth, depth)],
-            mate,
-        )
+        for at, n in ((half_rows, half_rows),) if part else ((0, half_rows // 2), (half_rows // 2, half_rows // 2)):
+            swaps.append(
+                send(
+                    x2.at[pl.ds(at, n), pl.ds(0, depth)],
+                    x2.at[pl.ds((at + half_rows) % n_rows, n), pl.ds(depth, depth)],
+                    mate,
+                )
+            )
 
     def gram(e, h, which, part):
         pair = mod4(pos[h][0] + 2) // 2
@@ -212,13 +216,15 @@
             second[e, h, w, dq].wait_recv()
             if dq in ahead:
                 hop[e, h, dq] = push(e, h, dp, dq, to)
-            if dq == 2:
+            if e == 1:
+                cross[e, h, dp, dq] = push(e, h, dp, dq, mate)
+            elif dq == 2:
                 push_strip(e, h, dp)
 
     def hops(e, h):
         for dq in (0, 1, 3, 2):
             hop[e, h, dq].wait_recv()
-        push_strip(e, h, 2)
+            cross[e, h, 2, dq] = push(e, h, 2, dq, mate)
 
     def place(e, cc, h, dp):
         p = mod4(pos[h][0] + dp)
@@ -236,7 +242,8 @@
                 g[pl.ds(row, EXTRA), pl.ds(ecol, STRIP)] = gs[1][cc, h, p, q, STRIP:]
 
     def place_mate(e, h, dp):
-        cross[e, h, dp].wait_recv()
+        for key in [k for k in cross if k[:3] == (e, h, dp)]:
+            cross[key].wait_recv()
         place(e, 1 - c, h, dp)
 
     def both(f, *args):
@@ -252,7 +259,7 @@
             else:
                 runs.append([k, k + 1])
         return sum(
-            jnp.dot(left[0:cols, lo * PAIR : hi * PAIR], g[lo * PAIR : hi * PAIR, n * PAIR : (n + 1) * PAIR], preferred_element_type=F32)
+            jnp.dot(left[:, lo * PAIR : hi * PAIR], g[lo * PAIR : hi * PAIR, n * PAIR : (n + 1) * PAIR], preferred_element_type=F32)
             for lo, hi in runs
         )
 
@@ -262,12 +269,13 @@
             for h in range(2):
                 gram(e, h, which, 0)
     for h in range(2):
-        swaps[1 - h].wait_recv()
+        swaps[h].wait_recv()
         gram(0, h, 0, 1)
         relay_out(0, h)
     for h in range(2):
         gram(0, h, 1, 1)
         plain_out(0, h)
+    swaps[2].wait_recv()
     for h in range(2):
         gram(1, h, 0, 1)
         relay_out(1, h)
@@ -277,37 +285,41 @@
         plain_out(1, h)
     both(merged_out, 1)
     both(ring2_first, 0)
+    both(ring2_first, 1)
     both(ring2_own, 0)
-    both(ring2_first, 1)
+    both(ring2_own, 1)
     both(gather_sides, 0)
     both(arrive, 0, 0)
     both(gather_far, 0)
-    both(ring2_own, 1)
+    both(gather_sides, 1)
+    both(gather_far, 1)
     both(arrive, 0, 1)
     both(arrive, 0, 3)
-    both(gather_sides, 1)
+    both(arrive, 1, 0)
     both(arrive, 0, 2)
-    both(arrive, 1, 0)
-    both(gather_far, 1)
     for h in range(2):
         for dp in (0, 3, 1):
             place(0, c, h, dp)
-    both(hops, 0)
+    both(place_mate, 0, 0)
     both(arrive, 1, 1)
     both(arrive, 1, 3)
-    for dp in (0, 3, 1):
-        both(place_mate, 0, dp)
+    both(place_mate, 0, 3)
+    both(place_mate, 0, 1)
+    for h in range(2):
+        place(1, c, h, 0)
+    both(place_mate, 1, 0)
+    both(hops, 0)
     for h in range(2):
         place(0, c, h, 2)
     both(arrive, 1, 2)
+    for h in range(2):
+        for dp in (3, 1):
+            place(1, c, h, dp)
     both(place_mate, 0, 2)
     for n in range(n_pairs):
-        yf[:, n * PAIR : (n + 1) * PAIR] = times_g(xt, n, range(n - 1, n + 2))
-    for h in range(2):
-        for dp in (0, 3, 1):
-            place(1, c, h, dp)
+        yf[:, n * PAIR : (n + 1) * PAIR] = times_g(x_ref, n, range(n - 1, n + 2))
     both(hops, 1)
-    for dp in (0, 3, 1):
+    for dp in (3, 1):
         both(place_mate, 1, dp)
     for h in range(2):
         place(1, c, h, 2)
@@ -315,24 +327,15 @@
     for uu in range(8):
         a, b = slice(uu * STRIP, (uu + 1) * STRIP), slice((uu + 8) * STRIP, (uu + 9) * STRIP)
         g[a, b] = g[b, a].T
+    scale = math.sqrt(FF)
     for n in range(n_pairs):
         at = slice(n * PAIR, (n + 1) * PAIR)
-        part = yf[:, at] + times_g(xt, n, range(n + 2, n + n_pairs - 1))
-        yf[:, at] = part
-        yb[:, at] = part.astype(BF16)
-    scale = math.sqrt(FF)
-    outs = []
+        part = yf[:, at] + times_g(x_ref, n, range(n + 2, n + n_pairs - 1))
+        yb[:, at] = (scale * coef_c * part).astype(BF16)
+        yf[:, at] = (scale * coef_a) * x_ref[:, at].astype(F32) + (scale * coef_b) * part
     for n in range(n_pairs):
         at = slice(n * PAIR, (n + 1) * PAIR)
-        part = times_g(yb, n, range(n_pairs))
-        updated = coef_a * xt[0:cols, at].astype(F32) + (coef_b * yf[:, at] + coef_c * part)
-        ob[:, at] = (scale * updated).astype(BF16)
-        lanes = pl.ds(n * PAIR, PAIR)
-        copy = pltpu.make_async_copy(ob.at[:, lanes], o_hbm.at[:, lanes], lsem.at[2 + n])
-        copy.start()
-        outs.append(copy)
-    for copy in outs:
-        copy.wait()
+        o_ref[:, at] = (yf[:, at] + times_g(yb, n, range(n_pairs))).astype(BF16)
     for copy in started:
         copy.wait_send()
 
@@ -341,18 +344,18 @@
     x = iterate.T
     cols, rows = x.shape
     depth = -(-cols // 128) * 128
-    copies = 2 + 4 * (6 + 3 + 3 + 12 + 4)
+    copies = 3 + 4 * (6 + 3 + 3 + 12 + 7) + 2 * 6
 
     def each(*dims, dtype=BF16):
         return [pltpu.VMEM((*dims, n, STRIP), dtype) for n in ROWS_OF]
 
     out = pl.pallas_call(
-        functools.partial(kernel, cols),
+        functools.partial(kernel, depth),
         out_shape=jax.ShapeDtypeStruct((cols, rows), BF16),
-        in_specs=[pl.BlockSpec(memory_space=pl.ANY)],
-        out_specs=pl.BlockSpec(memory_space=pl.ANY),
+        in_specs=[pl.BlockSpec(memory_space=pltpu.HBM)],
+        out_specs=pl.BlockSpec(memory_space=pltpu.VMEM),
         scratch_shapes=[
-            pltpu.VMEM((depth, rows), BF16),
+            pltpu.VMEM((cols, rows), BF16),
             pltpu.VMEM((rows, 2 * depth), BF16),
             *each(2, 4, 4, dtype=F32),
             *each(2, 3, 4),
@@ -365,13 +368,12 @@
             pltpu.VMEM((rows, rows), BF16),
             pltpu.VMEM((cols, rows), F32),
             pltpu.VMEM((cols, rows), BF16),
-            pltpu.VMEM((cols, rows), BF16),
             pltpu.SemaphoreType.DMA((copies,)),
             pltpu.SemaphoreType.DMA((copies,)),
-            pltpu.SemaphoreType.DMA((2 + rows // PAIR,)),
+            pltpu.SemaphoreType.DMA((2,)),
         ],
         compiler_params=pltpu.CompilerParams(
-            collective_id=0, has_side_effects=True, vmem_limit_bytes=60 * 1024 * 1024
+            collective_id=0, has_side_effects=True, vmem_limit_bytes=52 * 1024 * 1024
         ),
     )(x)
     return out.T

time: 58.5 us -> 53.5 us (0.915)
  Pallas kernels: 55.4 us -> 52.2 us
  local copies, waits for them, and re-layouts: 2.94 us -> 1.23 us
    pallas_call x1, Pallas kernels: 55.4 us -> 52.2 us  [body(): pl.pallas_call(functools.partial(kernel, depth), out_shape=jax.ShapeDtype...]
    unnamed x1, local copies, waits for them, and re-layouts: 2.94 us -> 1.23 us
where the time goes in v3:
time: 53.5 us; the launch traced here: 53.4 us
  Pallas kernels  52.2 us (98%)
  local copies, waits for them, and re-layouts  1.23 us (2%)
    pallas_call x1, Pallas kernels, body(): pl.pallas_call(functools.partial(kernel, depth), out_shape=jax.ShapeDtype...  52.2 us
    unnamed x1, local copies, waits for them, and re-layouts  1.23 us

profile of v3, /device:TPU:1, one launch (start us, length us, event | category | flops | bytes accessed | tf_op | source)
XLA Modules:
  0.0 53.4 jit_solution(2614260126306012698)
XLA Ops:
  0.0 52.2 %shard_map.17 = bf16[448,2048]{1,0:T(8,128)(2,1)S(1)} custom-call(bf16[448,2048]{1,0:T(8,128)(2,1)} %bitcast.3), custom_call_target="tpu_custom_call" | custom-call | tf_op jit(solution)/shard_map/pallas_call | solution.py:352
  52.2 1.2 %copy.3 = bf16[2048,448]{0,1:T(8,128)(2,1)} copy(bf16[2048,448]{0,1:T(8,128)(2,1)S(1)} %bitcast.2) | data formatting | bytes 3670016

commit v4 on v3

--- a/solution.py
+++ b/solution.py
@@ -51,6 +51,7 @@
     pos = ((y, z), (z, y))
     links = (((y_up, y_down), (z_up, z_down)), ((z_up, z_down), (y_up, y_down)))
     fars = ((y_far, z_far), (z_far, y_far))
+    sides = (dev(mod4(y + 1 + 2 * c), z, c), dev(y, mod4(z + 1 + 2 * c), c))
 
     count = [0]
     started = []
@@ -212,14 +213,16 @@
 
     def arrive(e, h, dq):
         up, down = links[h][0]
-        for w, dp, to, ahead in ((0, 3, up, (0, 1) if h == 0 else (1,)), (1, 1, down, (3,) if h == 0 else (0, 3))):
+        for w, dp, to, ahead in ((0, 3, up, 1), (1, 1, down, 3)):
             second[e, h, w, dq].wait_recv()
-            if dq in ahead:
+            if dq == ahead:
                 hop[e, h, dq] = push(e, h, dp, dq, to)
             if e == 1:
                 cross[e, h, dp, dq] = push(e, h, dp, dq, mate)
             elif dq == 2:
                 push_strip(e, h, dp)
+        if dq == 0:
+            hop[e, h, 0] = push(e, h, 3 - 2 * c, 0, sides[h])
 
     def hops(e, h):
         for dq in (0, 1, 3, 2):

time: 53.5 us -> 52.8 us (0.987)
  Pallas kernels: 52.2 us -> 51.5 us
    pallas_call x1, Pallas kernels: 52.2 us -> 51.5 us  [body(): pl.pallas_call(functools.partial(kernel, depth), out_shape=jax.ShapeDtype...]
where the time goes in v4:
time: 52.8 us; the launch traced here: 52.7 us
  Pallas kernels  51.5 us (98%)
  local copies, waits for them, and re-layouts  1.23 us (2%)
    pallas_call x1, Pallas kernels, body(): pl.pallas_call(functools.partial(kernel, depth), out_shape=jax.ShapeDtype...  51.5 us
    unnamed x1, local copies, waits for them, and re-layouts  1.23 us

profile of v4, /device:TPU:1, one launch (start us, length us, event | category | flops | bytes accessed | tf_op | source)
XLA Modules:
  0.0 52.7 jit_solution(2718257667077142128)
XLA Ops:
  0.0 51.5 %shard_map.17 = bf16[448,2048]{1,0:T(8,128)(2,1)S(1)} custom-call(bf16[448,2048]{1,0:T(8,128)(2,1)} %bitcast.3), custom_call_target="tpu_custom_call" | custom-call | tf_op jit(solution)/shard_map/pallas_call | solution.py:355
  51.5 1.2 %copy.3 = bf16[2048,448]{0,1:T(8,128)(2,1)} copy(bf16[2048,448]{0,1:T(8,128)(2,1)S(1)} %bitcast.2) | data formatting | bytes 3670016

commit v5 on v4

--- a/solution.py
+++ b/solution.py
@@ -52,6 +52,7 @@
     links = (((y_up, y_down), (z_up, z_down)), ((z_up, z_down), (y_up, y_down)))
     fars = ((y_far, z_far), (z_far, y_far))
     sides = (dev(mod4(y + 1 + 2 * c), z, c), dev(y, mod4(z + 1 + 2 * c), c))
+    backs = (dev(mod4(y + 3 - 2 * c), z, c), dev(y, mod4(z + 3 - 2 * c), c))
 
     count = [0]
     started = []
@@ -207,7 +208,8 @@
 
     def gather_far(e, h):
         first[e, h, 2].wait_recv()
-        hop[e, h, 2] = push(e, h, 0, 2, fars[h][0])
+        if e == 1:
+            hop[e, h, 2] = push(e, h, 0, 2, fars[h][0])
         push_near(e, h, 2)
         push_strip(e, h, 0)
 
@@ -223,6 +225,8 @@
                 push_strip(e, h, dp)
         if dq == 0:
             hop[e, h, 0] = push(e, h, 3 - 2 * c, 0, sides[h])
+        if dq == 2 and e == 0:
+            hop[e, h, 2] = push(e, h, 1 + 2 * c, 2, backs[h])
 
     def hops(e, h):
         for dq in (0, 1, 3, 2):

time: 52.8 us -> 52.4 us (level)
  no operation moved by 1% of the time
where the time goes in v5:
time: 52.4 us; the launch traced here: 52.3 us
  Pallas kernels  51 us (97%)
  local copies, waits for them, and re-layouts  1.23 us (2%)
    pallas_call x1, Pallas kernels, body(): pl.pallas_call(functools.partial(kernel, depth), out_shape=jax.ShapeDtype...  51 us
    unnamed x1, local copies, waits for them, and re-layouts  1.23 us

profile of v5, /device:TPU:1, one launch (start us, length us, event | category | flops | bytes accessed | tf_op | source)
XLA Modules:
  0.0 52.3 jit_solution(9326650169778280211)
XLA Ops:
  0.0 51.0 %shard_map.17 = bf16[448,2048]{1,0:T(8,128)(2,1)S(1)} custom-call(bf16[448,2048]{1,0:T(8,128)(2,1)} %bitcast.3), custom_call_target="tpu_custom_call" | custom-call | tf_op jit(solution)/shard_map/pallas_call | solution.py:359
  51.0 1.2 %copy.3 = bf16[2048,448]{0,1:T(8,128)(2,1)} copy(bf16[2048,448]{0,1:T(8,128)(2,1)S(1)} %bitcast.2) | data formatting | bytes 3670016
